TPU v7x, 32 devices: a whole 2x2x4 slice. The times are simulated.
32 devices in a mesh: occ: 4 (over y, x), vir: 8 (over z, core).
Axes of the slice: x: 2, y: 2, z: 4, core: 2. Of those that a mesh axis runs over, the one named last changes fastest.
Arguments:
- b_factors: float32 [32, 256, 4096], P('occ', 'vir'), may hold values from -0.6 to 0.6
- occ_energy: float32 [32], replicated, may hold values from -2 to -0.3
- vir_energy: float32 [256], replicated, may hold values from 0.2 to 3
Outputs:
- gamma: float32 [32, 256, 4096], P('occ', 'vir')
All inputs are finite; a program needn't handle non-finite values.
Results may differ from a plain program's by a relative error of at most 0.0003.
Values sent between devices are 32-bit elements; how exact they have to be, the bound alone decides.
A program may use at most 128 MiB of HBM per device.

v0:
```python
import functools

import jax
import jax.numpy as jnp
from jax import lax
from jax.experimental import pallas as pl
from jax.experimental.pallas import tpu as pltpu
from jax.sharding import PartitionSpec as P

MESH = pl.DeviceIdType.MESH
CHUNK = 512
AHEAD = 4
LAG = 2
STREAMS = 4


def split(value):
    high = value.astype(jnp.bfloat16)
    low = (value - high.astype(jnp.float32)).astype(jnp.bfloat16)
    return high, low


def product(a, b, contract):
    dims = ((contract[:1], contract[1:]), ((), ()))
    dot = functools.partial(lax.dot_general, dimension_numbers=dims, preferred_element_type=jnp.float32)
    (a_high, a_low), (b_high, b_low) = a, b
    return dot(a_high, b_high) + (dot(a_high, b_low) + dot(a_low, b_high))


def cols(k):
    return pl.ds(pl.multiple_of(k * CHUNK, CHUNK), CHUNK)


def every(count, body, first=0):
    def run(k, carry):
        body(k)
        return carry
    lax.fori_loop(first, count, run, 0)


def kernel(
    occ_count, vir_count, occ_block, vir_block,
    occ_ref, vir_ref, b_ref, total, land, amp_high, amp_low,
    own, own_high, own_low, sums, mine_gap, vir_row,
    own_sem, near_send, near_recv, far_send, far_recv, inner_send, inner_recv, outer_send, outer_recv,
):
    rows, width = b_ref.shape
    piece = rows // STREAMS
    occ_piece = occ_block // STREAMS
    chunks = width // CHUNK
    steps = STREAMS * chunks
    o = lax.axis_index("occ")
    v = lax.axis_index("vir")
    step = 1 - 2 * lax.rem(o, 2)
    partner = o + step
    relay_to = lax.rem(o + 2 * step + occ_count, occ_count)
    relay_from = lax.rem(o - 2 * step + occ_count, occ_count)
    across = lax.rem(o - step + occ_count, occ_count)
    turn = 1 - 2 * lax.rem(v, 2)
    v_inner = v + turn
    v_outer = lax.rem(v - turn + vir_count, vir_count)
    sources = ((partner, v), (o, v_inner), (o, v_outer), (across, v))

    def sent(k):
        return b_ref.at[pl.ds(pl.multiple_of(k // chunks * piece, piece), piece), cols(k % chunks)]

    def landed(k, stream):
        return land.at[k // chunks, pl.ds(stream * piece, piece), cols(k % chunks)]

    def remote(k, source, stream, send_sem, recv_sem, device):
        return pltpu.make_async_remote_copy(
            source, landed(k, stream), send_sem.at[k], recv_sem.at[k], device_id=device, device_id_type=MESH)

    def load(k):
        return pltpu.make_async_copy(b_ref.at[:, cols(k)], own.at[:, cols(k)], own_sem.at[k])

    def near_copy(k):
        return remote(k, sent(k), 0, near_send, near_recv, (partner, v))

    def inner_copy(k):
        return remote(k, sent(k), 1, inner_send, inner_recv, (o, v_inner))

    def outer_copy(k):
        return remote(k, sent(k), 2, outer_send, outer_recv, (o, v_outer))

    def far_copy(k):
        return remote(k, landed(k, 0), 3, far_send, far_recv, (relay_to, v))

    def send(k):
        near_copy(k).start()
        outer_copy(k).start()
        inner_copy(k).start()

    barrier = pltpu.get_barrier_semaphore()
    for device in ((partner, v), (relay_to, v), (relay_from, v), (o, v_inner), (o, v_outer)):
        pl.semaphore_signal(barrier, inc=1, device_id=device, device_id_type=MESH)
    pl.semaphore_wait(barrier, 5)
    every(AHEAD, send)
    every(chunks, lambda k: load(k).start())

    lane = lax.broadcasted_iota(jnp.int32, (8, rows), 1)
    within = lane
    for i in range(1, occ_block):
        within = within - jnp.where(lane >= i * vir_block, vir_block, 0)

    def vir_values(blocks):
        values = jnp.zeros((8, rows), jnp.float32)
        for stream, block in enumerate(blocks):
            part = values
            for a in range(vir_block):
                part = jnp.where(within == a, vir_ref[block * vir_block + a], part)
            values = jnp.where(lane >= stream * piece, part, values)
        return values

    def occ_values(places):
        values = jnp.zeros((8, rows), jnp.float32)
        for i, place in enumerate(places):
            values = jnp.where(lane >= i * vir_block, occ_ref[place], values)
        return values

    def whole(row):
        return jnp.broadcast_to(row[:1], (rows, rows))

    own_row = occ_values([o * occ_block + i for i in range(occ_block)]) - vir_values([v])
    mine_gap[...] = whole(own_row).T
    vir_row[...] = vir_values([block for _, block in sources])

    def gather(block, k):
        a = (own_high[:, cols(k)], own_low[:, cols(k)])
        sums[...] += product(a, split(block), (1, 1))

    def amplitude(row):
        amp_high[...], amp_low[...] = split(sums[...] / (mine_gap[...] + whole(row)))
        sums[...] = jnp.zeros_like(sums)

    def spread(block):
        return product((amp_high[...], amp_low[...]), split(block), (1, 0))

    sums[...] = jnp.zeros_like(sums)

    def own_chunk(k):
        load(k).wait()
        high, low = split(own[:, cols(k)])
        own_high[:, cols(k)] = high
        own_low[:, cols(k)] = low
        gather(own[:, cols(k)], k)

    every(chunks, own_chunk)
    amplitude(own_row)

    def own_spread(k):
        total[:, cols(k)] = spread(own[:, cols(k)])

    def read(k):
        phase, here = k // chunks, k % chunks
        near_copy(k).wait_send()
        inner_copy(k).wait()
        outer_copy(k).wait()
        far_copy(k).wait()
        gather(land[phase, :, cols(here)], here)

        @pl.when(phase == 0)
        def _():
            own_spread(here)

        @pl.when(phase > 0)
        def _():
            total[:, cols(here)] += spread(land[jnp.maximum(phase - 1, 0), :, cols(here)])

        @pl.when(here == chunks - 1)
        def _():
            places = [
                block * occ_block + phase * occ_piece + i for block, _ in sources for i in range(occ_piece)]
            amplitude(occ_values(places) - vir_row[...])

    def arrive(k):
        near_copy(k).wait_recv()
        far_copy(k).start()

        @pl.when(k + AHEAD < steps)
        def _():
            send(k + AHEAD)

        @pl.when(k >= LAG)
        def _():
            read(k - LAG)

    every(steps, arrive)
    every(steps, read, steps - LAG)


def finish(total, land, amp_high, amp_low, out_ref, done, out_sem):
    amp = (amp_high[...], amp_low[...])
    chunks = total.shape[1] // CHUNK

    def store(k):
        return pltpu.make_async_copy(done.at[:, cols(k)], out_ref.at[:, cols(k)], out_sem.at[k])

    def tile(k):
        done[:, cols(k)] = total[:, cols(k)] + product(amp, split(land[STREAMS - 1, :, cols(k)]), (1, 0))
        store(k).start()

    every(chunks, tile)
    every(chunks, lambda k: store(k).wait())


def local(b_factors, occ_energy, vir_energy):
    occ_block, vir_block, width = b_factors.shape
    occ_count = lax.axis_size("occ")
    vir_count = lax.axis_size("vir")
    rows = occ_block * vir_block
    chunks = width // CHUNK
    steps = STREAMS * chunks
    block = pltpu.VMEM((rows, width), jnp.float32)
    half = pltpu.VMEM((rows, width), jnp.bfloat16)
    square = pltpu.VMEM((rows, rows), jnp.float32)
    vmem = pl.BlockSpec(memory_space=pltpu.VMEM)
    smem = pl.BlockSpec(memory_space=pltpu.SMEM)
    hbm = pl.BlockSpec(memory_space=pl.ANY)
    sems = [pltpu.SemaphoreType.DMA((count,)) for count in [chunks] + [steps] * 8]
    parts = pl.pallas_call(
        functools.partial(kernel, occ_count, vir_count, occ_block, vir_block),
        out_shape=[
            block,
            pltpu.VMEM((STREAMS, rows, width), jnp.float32),
            pltpu.VMEM((rows, rows), jnp.bfloat16),
            pltpu.VMEM((rows, rows), jnp.bfloat16),
        ],
        in_specs=[smem, smem, hbm],
        out_specs=[vmem] * 4,
        scratch_shapes=[block, half, half, square, square, pltpu.VMEM((8, rows), jnp.float32)] + sems,
        compiler_params=pltpu.CompilerParams(
            collective_id=0, has_side_effects=True, vmem_limit_bytes=42 * 2**20),
    )(occ_energy, vir_energy, b_factors.reshape(rows, width))
    out = pl.pallas_call(
        finish,
        out_shape=jax.ShapeDtypeStruct((rows, width), jnp.float32),
        in_specs=[vmem] * 4,
        out_specs=hbm,
        scratch_shapes=[block, pltpu.SemaphoreType.DMA((chunks,))],
        compiler_params=pltpu.CompilerParams(vmem_limit_bytes=10 * 2**20),
    )(*parts)
    return out.reshape(occ_block, vir_block, width)


def solution(mesh):
    in_specs = (P("occ", "vir", None), P(), P())
    out_specs = P("occ", "vir", None)
    return jax.shard_map(local, mesh=mesh, in_specs=in_specs, out_specs=out_specs, check_vma=False)
```

profile of v0, /device:TPU:0, one launch (start us, length us, event | category | flops | bytes accessed | tf_op | source)
XLA Modules:
  0.0 108.7 jit_solution(11886499795241613453)
XLA Ops:
  0.0 104.7 %shard_map.37 = (f32[256,4096]{1,0:T(8,128)S(1)}, f32[4,256,4096]{2,1,0:T(8,128)S(1)}, bf16[256,256]{1,0:T(8,128)(2,1)S(1)}, bf16[256,256]{1,0:T(8,128)(2,1)S(1)}) custom-call(f32[32]{0:T(128)} %occ_ref.1, f32[256]{0:T(256)} %vir_ref.1, f32[256,4096]{1,0:T(8,128)} %bitcast.2), custom_call_target="tpu_custom_call" | custom-call | tf_op jit(solution)/shard_map/pallas_call | solution.py:221
  104.7 4.0 %shard_map.38 = f32[256,4096]{1,0:T(8,128)} custom-call(f32[256,4096]{1,0:T(8,128)S(1)} %get-tuple-element.9.total, f32[4,256,4096]{2,1,0:T(8,128)S(1)} %get-tuple-element.10.land, bf16[256,256]{1,0:T(8,128)(2,1)S(1)} %get-tuple-element.11.amp_high, bf16[256,256]{1,0:T(8,128)(2,1)S(1)} %get-tuple-element.12.amp_low), custom_call_target="tpu_custom_call" | custom-call | tf_op jit(solution)/shard_map/pallas_call | solution.py:235
where the time goes:
time: 109 us
  Pallas kernels  109 us (100%)
    pallas_call x1, Pallas kernels, local(): pl.pallas_call(functools.partial(kernel, occ_count, vir_count, occ_block,...  105 us
    pallas_call x1, Pallas kernels, local(): pl.pallas_call(finish, out_shape=jax.ShapeDtypeStruct((rows, width), jnp....  4.02 us

commit v1 on v0

v1 whole, which is shorter than its diff:
```python
import functools

import jax
import jax.numpy as jnp
from jax import lax
from jax.experimental import pallas as pl
from jax.experimental.pallas import tpu as pltpu
from jax.sharding import PartitionSpec as P

MESH = pl.DeviceIdType.MESH
CHUNK = 512
STREAMS = 4
SHARES = (4, 4, 4, 8, 16, 16)
LAGS = (2, 2, 2, 3, 6, 6)
RELAY_ROWS = 32
WIDE = 2
DEPTH = 256
STACK = 4


def phases(rows):
    out, base = [], 0
    for share in SHARES:
        count = rows // share
        lanes = STREAMS * count
        out.append((base, count, STACK if STACK * lanes <= DEPTH else 1))
        base += count
    assert base == rows
    return out


def split(value):
    high = value.astype(jnp.bfloat16)
    low = (value - high.astype(jnp.float32)).astype(jnp.bfloat16)
    return high, low


def dot(a, b, contract):
    dims = ((contract[:1], contract[1:]), ((), ()))
    return lax.dot_general(a, b, dimension_numbers=dims, preferred_element_type=jnp.float32)


def product(a, b, contract):
    (a_high, a_low), (b_high, b_low) = a, b
    return dot(a_high, b_high, contract) + (dot(a_high, b_low, contract) + dot(a_low, b_high, contract))


def stacked(amp, block):
    high, low = split(block)
    return dot(amp, jnp.concatenate([high, low] * (STACK // 2), axis=0), (1, 0))


def cols(k, wide=1):
    size = wide * CHUNK
    return pl.ds(pl.multiple_of(k * size, size), size)


def every(count, body, first=0):
    def run(k, carry):
        body(k)
        return carry
    lax.fori_loop(first, count, run, 0)


def kernel(
    occ_count, vir_count, occ_block, vir_block,
    occ_ref, vir_ref, b_ref, total, land, amp_high,
    amp_low, own, own_high, own_low, sums, mine_gap, gaps,
    own_sem, near_send, far_send, inner_send, outer_send, near_recv, far_recv, inner_recv, outer_recv,
):
    rows, width = b_ref.shape
    plan = phases(rows)
    chunks = width // CHUNK
    o = lax.axis_index("occ")
    v = lax.axis_index("vir")
    step = 1 - 2 * lax.rem(o, 2)
    partner = o + step
    relay_to = lax.rem(o + 2 * step + occ_count, occ_count)
    relay_from = lax.rem(o - 2 * step + occ_count, occ_count)
    across = lax.rem(o - step + occ_count, occ_count)
    turn = 1 - 2 * lax.rem(v, 2)
    v_inner = v + turn
    v_outer = lax.rem(v - turn + vir_count, vir_count)
    sources = ((partner, v), (o, v_inner), (o, v_outer), (across, v))
    pieces = [max(1, count // RELAY_ROWS) for _, count, _ in plan]
    near_first = [sum(pieces[:p]) * chunks for p in range(len(plan))]

    def mine(p, i, count, where):
        return b_ref.at[pl.ds(plan[p][0] + i * count, count), where]

    def landed(p, stream, i, count, where):
        return land.at[pl.ds(STREAMS * plan[p][0] + stream * plan[p][1] + i * count, count), where]

    def remote(source, target, send_sem, recv_sem, device):
        return pltpu.make_async_remote_copy(
            source, target, send_sem, recv_sem, device_id=device, device_id_type=MESH)

    def near_copy(p, k, i):
        count = plan[p][1] // pieces[p]
        return remote(
            mine(p, i, count, cols(k)), landed(p, 0, i, count, cols(k)),
            near_send, near_recv.at[near_first[p] + k * pieces[p] + i], (partner, v))

    def far_copy(p, k, i, count):
        return remote(
            landed(p, 0, i, count, cols(k)), landed(p, 3, i, count, cols(k)),
            far_send, far_recv.at[p * chunks + k], (relay_to, v))

    def inner_copy(p):
        count = plan[p][1]
        return remote(
            mine(p, 0, count, slice(None)), landed(p, 1, 0, count, slice(None)),
            inner_send, inner_recv.at[p], (o, v_inner))

    def outer_copy(p, c):
        count = plan[p][1]
        return remote(
            mine(p, 0, count, cols(c, WIDE)), landed(p, 2, 0, count, cols(c, WIDE)),
            outer_send, outer_recv.at[p * (chunks // WIDE) + c], (o, v_outer))

    def load(k):
        return pltpu.make_async_copy(b_ref.at[:, cols(k)], own.at[:, cols(k)], own_sem.at[k])

    def send(p):
        def body(c):
            for k in range(WIDE):
                for i in range(pieces[p]):
                    near_copy(p, WIDE * c + k, i).start()
            outer_copy(p, c).start()
        every(chunks // WIDE, body)
        inner_copy(p).start()

    barrier = pltpu.get_barrier_semaphore()
    for device in ((partner, v), (relay_to, v), (relay_from, v), (o, v_inner), (o, v_outer)):
        pl.semaphore_signal(barrier, inc=1, device_id=device, device_id_type=MESH)
    pl.semaphore_wait(barrier, 5)
    send(0)
    every(chunks, lambda k: load(k).start())
    for p in range(1, len(plan)):
        send(p)

    lane = lax.broadcasted_iota(jnp.int32, (8, rows), 1)

    def gap_row(base, count, blocks):
        part = min(count, vir_block)
        within = lax.rem(lane, part)
        virs = jnp.zeros((8, rows), jnp.float32)
        occs = virs
        for stream, (occ, vir) in enumerate(blocks):
            row = virs
            for a in range(part):
                row = jnp.where(within == a, vir_ref[vir * vir_block + base % vir_block + a], row)
            virs = jnp.where(lane >= stream * count, row, virs)
            for i in range(count // part):
                occs = jnp.where(
                    lane >= stream * count + i * part, occ_ref[occ * occ_block + base // vir_block + i], occs)
        return occs - virs

    def whole(row):
        return jnp.broadcast_to(row[:1], (rows, rows))

    own_row = gap_row(0, rows, [(o, v)])
    mine_gap[...] = whole(own_row).T

    def gather(block, k, copies=1):
        lanes = copies * block.shape[0]
        a = (own_high[:, cols(k)], own_low[:, cols(k)])
        b = [jnp.concatenate([part] * copies, axis=0) if copies > 1 else part for part in split(block)]
        sums[:, :lanes] += product(a, b, (1, 1))

    def amplitude(row, lanes, copies=1):
        value = sums[:, :lanes] / (mine_gap[:, :lanes] + whole(row)[:, :lanes])
        high, low = split(value)
        if copies > 1:
            place = lax.rem(lax.broadcasted_iota(jnp.int32, (rows, lanes), 1), lanes)
            wide = high.astype(jnp.float32)
            amp_high[:, :lanes] = jnp.where(place < lanes // 2, wide, value - wide).astype(jnp.bfloat16)
        else:
            amp_high[:, :lanes] = high
            amp_low[:, :lanes] = low
        sums[...] = jnp.zeros_like(sums)

    def spread(block, copies=1):
        lanes = copies * block.shape[0]
        if copies > 1:
            return stacked(amp_high[:, :lanes], block)
        return product((amp_high[:, :lanes], amp_low[:, :lanes]), split(block), (1, 0))

    sums[...] = jnp.zeros_like(sums)

    def own_chunk(k):
        load(k).wait()
        high, low = split(own[:, cols(k)])
        own_high[:, cols(k)] = high
        own_low[:, cols(k)] = low
        gather(own[:, cols(k)], k)

    def block(p, k):
        return land[pl.ds(STREAMS * plan[p][0], STREAMS * plan[p][1]), cols(k)]

    def read_first(p, k):
        if p == 0:
            total[:, cols(k)] = spread(own[:, cols(k)])
        else:
            total[:, cols(k)] += spread(block(p - 1, k), plan[p - 1][2])

    def read_second(p, k):
        far_copy(p, k, 0, plan[p][1]).wait_recv()

        @pl.when(lax.rem(k, WIDE) == 0)
        def _():
            outer_copy(p, k // WIDE).wait_recv()
        gather(block(p, k), k, plan[p][2])

    def finished(p):
        _, count, copies = plan[p]
        amplitude(gaps[p], copies * STREAMS * count, copies)

    def relay(p, k, i):
        near_copy(p, k, i).wait_recv()
        far_copy(p, k, i, plan[p][1] // pieces[p]).start()

    def arrive(p, k, first=None, second=None):
        for i in range(pieces[p]):
            relay(p, k, i)
            if i == 0 and first is not None:
                first()
        if second is not None:
            second()

    half = chunks // 2
    every(half, own_chunk)
    quarter = half + chunks // 4
    arrive(0, 0, lambda: every(quarter, own_chunk, half), lambda: every(chunks, own_chunk, quarter))
    amplitude(own_row, rows)
    for p, (base, count, copies) in enumerate(plan):
        gaps[p] = gap_row(base, count, list(sources) * copies)

    done, runs = 0, []
    for p in range(len(plan)):
        for k in range(1 if p == 0 else 0, chunks):
            due = p * chunks + k - LAGS[p]
            task = None
            if due >= done:
                task = done // chunks, done % chunks - k
                done += 1
            if runs and runs[-1][0] == p and runs[-1][3] == task:
                runs[-1][2] = k + 1
            else:
                runs.append([p, k, k + 1, task])

    for p, first, end, task in runs:
        if task is None:
            every(end, lambda k, p=p: arrive(p, k), first)
            continue
        q, shift = task
        if first + shift == 0:
            inner_copy(q).wait_recv()
        every(end, lambda k, p=p, q=q, shift=shift: arrive(
            p, k, lambda: read_first(q, k + shift), lambda: read_second(q, k + shift)), first)
        if end + shift == chunks:
            finished(q)

    while done < len(plan) * chunks:
        q, first = done // chunks, done % chunks
        if first == 0:
            inner_copy(q).wait_recv()

        def rest(k, q=q):
            read_first(q, k)
            read_second(q, k)
        every(chunks, rest, first)
        finished(q)
        done = (q + 1) * chunks

    sent = land.at[pl.ds(0, rows), :]
    remote(b_ref, sent, near_send, near_recv.at[0], (partner, v)).wait_send()
    remote(b_ref, sent, inner_send, inner_recv.at[0], (o, v_inner)).wait_send()
    remote(b_ref, sent, outer_send, outer_recv.at[0], (o, v_outer)).wait_send()
    remote(sent, sent, far_send, far_recv.at[0], (relay_to, v)).wait_send()


def finish(total, land, amp, out_ref, done, out_sem):
    rows, width = total.shape
    base, count, copies = phases(rows)[-1]
    chunks = width // CHUNK
    lanes = copies * STREAMS * count

    def store(k):
        return pltpu.make_async_copy(done.at[:, cols(k)], out_ref.at[:, cols(k)], out_sem.at[k])

    def tile(k):
        block = land[pl.ds(STREAMS * base, STREAMS * count), cols(k)]
        done[:, cols(k)] = total[:, cols(k)] + stacked(amp[:, :lanes], block)
        store(k).start()

    every(chunks, tile)
    every(chunks, lambda k: store(k).wait())


def local(b_factors, occ_energy, vir_energy):
    occ_block, vir_block, width = b_factors.shape
    occ_count = lax.axis_size("occ")
    vir_count = lax.axis_size("vir")
    rows = occ_block * vir_block
    plan = phases(rows)
    chunks = width // CHUNK
    near = sum(max(1, count // RELAY_ROWS) for _, count, _ in plan) * chunks
    block = pltpu.VMEM((rows, width), jnp.float32)
    half = pltpu.VMEM((rows, width), jnp.bfloat16)
    square = pltpu.VMEM((rows, rows), jnp.float32)
    amp = pltpu.VMEM((rows, rows), jnp.bfloat16)
    vmem = pl.BlockSpec(memory_space=pltpu.VMEM)
    smem = pl.BlockSpec(memory_space=pltpu.SMEM)
    hbm = pl.BlockSpec(memory_space=pl.ANY)
    sems = [pltpu.SemaphoreType.DMA((chunks,))] + [pltpu.SemaphoreType.DMA] * 4 + [
        pltpu.SemaphoreType.DMA((count,))
        for count in (near, len(plan) * chunks, len(plan), len(plan) * chunks // WIDE)]
    parts = pl.pallas_call(
        functools.partial(kernel, occ_count, vir_count, occ_block, vir_block),
        out_shape=[block, pltpu.VMEM((STREAMS * rows, width), jnp.float32), amp],
        in_specs=[smem, smem, hbm],
        out_specs=[vmem] * 3,
        scratch_shapes=[
            amp, block, half, half, square, square, pltpu.VMEM((len(plan), 8, rows), jnp.float32)] + sems,
        compiler_params=pltpu.CompilerParams(
            collective_id=0, has_side_effects=True, vmem_limit_bytes=42 * 2**20),
    )(occ_energy, vir_energy, b_factors.reshape(rows, width))
    out = pl.pallas_call(
        finish,
        out_shape=jax.ShapeDtypeStruct((rows, width), jnp.float32),
        in_specs=[vmem] * 3,
        out_specs=hbm,
        scratch_shapes=[block, pltpu.SemaphoreType.DMA((chunks,))],
        compiler_params=pltpu.CompilerParams(vmem_limit_bytes=10 * 2**20),
    )(*parts)
    return out.reshape(occ_block, vir_block, width)


def solution(mesh):
    in_specs = (P("occ", "vir", None), P(), P())
    out_specs = P("occ", "vir", None)
    return jax.shard_map(local, mesh=mesh, in_specs=in_specs, out_specs=out_specs, check_vma=False)
```

time: 109 us -> 110 us (level)
    pallas_call x1, Pallas kernels: 105 us -> 107 us  [local(): pl.pallas_call(functools.partial(kernel, occ_count, vir_count, occ_block,...]
    pallas_call x1, Pallas kernels: 4.02 us -> 2.72 us  [local(): pl.pallas_call(finish, out_shape=jax.ShapeDtypeStruct((rows, width), jnp....]
where the time goes in v1:
time: 110 us
  Pallas kernels  110 us (100%)
    pallas_call x1, Pallas kernels, local(): pl.pallas_call(functools.partial(kernel, occ_count, vir_count, occ_block,...  107 us
    pallas_call x1, Pallas kernels, local(): pl.pallas_call(finish, out_shape=jax.ShapeDtypeStruct((rows, width), jnp....  2.72 us

profile of v1, /device:TPU:0, one launch (start us, length us, event | category | flops | bytes accessed | tf_op | source)
XLA Modules:
  0.0 109.9 jit_solution(8120399089967815768)
XLA Ops:
  0.0 107.2 %shard_map.37 = (f32[256,4096]{1,0:T(8,128)S(1)}, f32[1024,4096]{1,0:T(8,128)S(1)}, bf16[256,256]{1,0:T(8,128)(2,1)S(1)}) custom-call(f32[32]{0:T(128)} %occ_ref.1, f32[256]{0:T(256)} %vir_ref.1, f32[256,4096]{1,0:T(8,128)} %bitcast.2), custom_call_target="tpu_custom_call" | custom-call | tf_op jit(solution)/shard_map/pallas_call | solution.py:319
  107.2 2.7 %shard_map.38 = f32[256,4096]{1,0:T(8,128)} custom-call(f32[256,4096]{1,0:T(8,128)S(1)} %get-tuple-element.8.total, f32[1024,4096]{1,0:T(8,128)S(1)} %get-tuple-element.9.land, bf16[256,256]{1,0:T(8,128)(2,1)S(1)} %get-tuple-element.10.amp), custom_call_target="tpu_custom_call" | custom-call | tf_op jit(solution)/shard_map/pallas_call | solution.py:329

commit v2 on v1

v2 whole, which is shorter than its diff:
```python
import functools

import jax
import jax.numpy as jnp
from jax import lax
from jax.experimental import pallas as pl
from jax.experimental.pallas import tpu as pltpu
from jax.sharding import PartitionSpec as P

MESH = pl.DeviceIdType.MESH
CHUNK = 512
STREAMS = 4
SHARES = (4, 4, 4, 8, 8)
LAG = 3
RELAY_ROWS = 16
AHEAD = 8
WIDE = 2
DEPTH = 256


def phases(rows):
    out, base = [], 0
    for share in SHARES:
        out.append((base, rows // share))
        base += rows // share
    assert base == rows
    return out


def split(value):
    high = value.astype(jnp.bfloat16)
    low = (value - high.astype(jnp.float32)).astype(jnp.bfloat16)
    return high, low


def dot(a, b, contract):
    dims = ((contract[:1], contract[1:]), ((), ()))
    return lax.dot_general(a, b, dimension_numbers=dims, preferred_element_type=jnp.float32)


def product(a, b, contract):
    (a_high, a_low), (b_high, b_low) = a, b
    return dot(a_high, b_high, contract) + (dot(a_high, b_low, contract) + dot(a_low, b_high, contract))


def spread(amp_high, amp_low, block):
    count = block.shape[0]
    high, low = split(block)
    if 2 * count <= DEPTH:
        return dot(amp_high[:, :2 * count], jnp.concatenate([high, high], axis=0), (1, 0)) + dot(
            amp_high[:, :count], low, (1, 0))
    return product((amp_high[:, :count], amp_low[:, :count]), (high, low), (1, 0))


def cols(k, wide=1):
    size = wide * CHUNK
    return pl.ds(pl.multiple_of(k * size, size), size)


def every(count, body, first=0):
    def run(k, carry):
        body(k)
        return carry
    lax.fori_loop(first, count, run, 0)


def kernel(
    occ_count, vir_count, occ_block, vir_block,
    occ_ref, vir_ref, b_ref, total, land, amp_high, amp_low,
    own, own_high, own_low, sums, mine_gap, gaps,
    own_sem, near_send, far_send, inner_send, outer_send, near_recv, far_recv, inner_recv, outer_recv,
):
    rows, width = b_ref.shape
    plan = phases(rows)
    chunks = width // CHUNK
    o = lax.axis_index("occ")
    v = lax.axis_index("vir")
    step = 1 - 2 * lax.rem(o, 2)
    partner = o + step
    relay_to = lax.rem(o + 2 * step + occ_count, occ_count)
    relay_from = lax.rem(o - 2 * step + occ_count, occ_count)
    across = lax.rem(o - step + occ_count, occ_count)
    turn = 1 - 2 * lax.rem(v, 2)
    v_inner = v + turn
    v_outer = lax.rem(v - turn + vir_count, vir_count)
    sources = ((partner, v), (o, v_inner), (o, v_outer), (across, v))
    pieces = [count // RELAY_ROWS for _, count in plan]
    pairs = [WIDE if count > min(c for _, c in plan) else 1 for _, count in plan]
    far_first = [sum(chunks // pair for pair in pairs[:p]) for p in range(len(plan))]

    def mine(p, i, count, where):
        return b_ref.at[pl.ds(plan[p][0] + i * count, count), where]

    def landed(p, stream, i, count, where):
        return land.at[pl.ds(STREAMS * plan[p][0] + stream * plan[p][1] + i * count, count), where]

    def remote(source, target, send_sem, recv_sem, device):
        return pltpu.make_async_remote_copy(
            source, target, send_sem, recv_sem, device_id=device, device_id_type=MESH)

    def near_copy(p, k, i):
        return remote(
            mine(p, i, RELAY_ROWS, cols(k)), landed(p, 0, i, RELAY_ROWS, cols(k)),
            near_send, near_recv.at[lax.rem(k * pieces[p] + i, 2 * AHEAD)], (partner, v))

    def far_copy(p, k, i):
        return remote(
            landed(p, 0, i, RELAY_ROWS, cols(k)), landed(p, 3, i, RELAY_ROWS, cols(k)),
            far_send, far_recv.at[far_first[p] + k // pairs[p]], (relay_to, v))

    def far_here(p, c):
        where = cols(c, pairs[p])
        return remote(
            landed(p, 0, 0, plan[p][1], where), landed(p, 3, 0, plan[p][1], where),
            far_send, far_recv.at[far_first[p] + c], (relay_to, v))

    def inner_copy(p):
        count = plan[p][1]
        return remote(
            mine(p, 0, count, slice(None)), landed(p, 1, 0, count, slice(None)),
            inner_send, inner_recv.at[p], (o, v_inner))

    def outer_copy(p, c):
        count = plan[p][1]
        return remote(
            mine(p, 0, count, cols(c, WIDE)), landed(p, 2, 0, count, cols(c, WIDE)),
            outer_send, outer_recv.at[p * (chunks // WIDE) + c], (o, v_outer))

    def load(k):
        return pltpu.make_async_copy(b_ref.at[:, cols(k, WIDE)], own.at[:, cols(k, WIDE)], own_sem.at[k])

    barrier = pltpu.get_barrier_semaphore()
    for device in ((partner, v), (relay_to, v), (relay_from, v), (o, v_inner), (o, v_outer)):
        pl.semaphore_signal(barrier, inc=1, device_id=device, device_id_type=MESH)
    pl.semaphore_wait(barrier, 5)
    for n in range(AHEAD):
        near_copy(0, n // pieces[0], n % pieces[0]).start()
    for p in range(len(plan)):
        every(chunks // WIDE, lambda c: outer_copy(p, c).start())
        inner_copy(p).start()
        if p == 0:
            every(chunks // WIDE, lambda k: load(k).start())

    lane = lax.broadcasted_iota(jnp.int32, (8, rows), 1)

    def gap_row(base, count, blocks):
        part = min(count, vir_block)
        within = lax.rem(lane, part)
        virs = jnp.zeros((8, rows), jnp.float32)
        occs = virs
        for stream, (occ, vir) in enumerate(blocks):
            row = virs
            for a in range(part):
                row = jnp.where(within == a, vir_ref[vir * vir_block + base % vir_block + a], row)
            virs = jnp.where(lane >= stream * count, row, virs)
            for i in range(count // part):
                occs = jnp.where(
                    lane >= stream * count + i * part, occ_ref[occ * occ_block + base // vir_block + i], occs)
        return occs - virs

    def whole(row):
        return jnp.broadcast_to(row[:1], (rows, rows))

    own_row = gap_row(0, rows, [(o, v)])
    mine_gap[...] = whole(own_row).T

    def gather(block, k):
        count = block.shape[0]
        mine = (own_high[:, cols(k)], own_low[:, cols(k)])
        sums[:, :count] += product(mine, split(block), (1, 1))

    def amplitude(row, count):
        value = sums[:, :count] / (mine_gap[:, :count] + whole(row)[:, :count])
        high, low = split(value)
        amp_high[:, :count] = high
        if 2 * count <= DEPTH:
            amp_high[:, count:2 * count] = low
        else:
            amp_low[:, :count] = low
        sums[...] = jnp.zeros_like(sums)

    sums[...] = jnp.zeros_like(sums)

    def own_chunk(k):
        @pl.when(lax.rem(k, WIDE) == 0)
        def _():
            load(k // WIDE).wait()
        high, low = split(own[:, cols(k)])
        own_high[:, cols(k)] = high
        own_low[:, cols(k)] = low
        gather(own[:, cols(k)], k)

    def block(p, k):
        return land[pl.ds(STREAMS * plan[p][0], STREAMS * plan[p][1]), cols(k)]

    def read_first(p, k):
        if p == 0:
            total[:, cols(k)] = spread(amp_high, amp_low, own[:, cols(k)])
        else:
            total[:, cols(k)] += spread(amp_high, amp_low, block(p - 1, k))

    def read_second(p, k):
        if pairs[p] == 1:
            far_here(p, k).wait_recv()

        @pl.when(lax.rem(k, WIDE) == 0)
        def _():
            if pairs[p] == WIDE:
                far_here(p, k // WIDE).wait_recv()
            outer_copy(p, k // WIDE).wait_recv()
        gather(block(p, k), k)

    def finished(p):
        amplitude(gaps[p], STREAMS * plan[p][1])

    def relay(p, k, i):
        near_copy(p, k, i).wait_recv()
        far_copy(p, k, i).start()
        later = chunks - AHEAD // pieces[p]

        @pl.when(k < later)
        def _():
            near_copy(p, k + AHEAD // pieces[p], i).start()

        if p + 1 < len(plan):
            ratio = pieces[p] // pieces[p + 1]

            @pl.when(k >= later)
            def _():
                near_copy(p + 1, (k - later) * ratio + i // pieces[p + 1], i % pieces[p + 1]).start()

    def arrive(p, k, work):
        for i in range(pieces[p]):
            relay(p, k, i)
            if i < len(work):
                work[i]()

    def fill(p):
        gaps[p] = gap_row(plan[p][0], plan[p][1], sources)

    assert pieces[0] == 4 and len(plan) == 5
    half = chunks // 2
    every(half, own_chunk)
    arrive(0, 0, [functools.partial(every, half + n + 1, own_chunk, half + n) for n in range(half)])
    arrive(0, 1, [lambda: amplitude(own_row, rows), lambda: fill(0), lambda: fill(1)])
    arrive(0, 2, [lambda: fill(2), lambda: fill(3), lambda: fill(4)])

    done, runs = 0, []
    for p in range(len(plan)):
        for k in range(LAG if p == 0 else 0, chunks):
            due = p * chunks + k - LAG
            task = None
            if due >= done:
                task = done // chunks, done % chunks - k
                done += 1
            if runs and runs[-1][0] == p and runs[-1][3] == task:
                runs[-1][2] = k + 1
            else:
                runs.append([p, k, k + 1, task])

    for p, first, end, task in runs:
        if task is None:
            every(end, lambda k, p=p: arrive(p, k, []), first)
            continue
        q, shift = task
        if first + shift == 0:
            inner_copy(q).wait_recv()
        every(end, lambda k, p=p, q=q, shift=shift: arrive(
            p, k, [lambda: read_first(q, k + shift), lambda: read_second(q, k + shift)]), first)
        if end + shift == chunks:
            finished(q)

    while done < len(plan) * chunks:
        q, first = done // chunks, done % chunks
        if first == 0:
            inner_copy(q).wait_recv()

        def rest(k, q=q):
            read_first(q, k)
            read_second(q, k)
        every(chunks, rest, first)
        finished(q)
        done = (q + 1) * chunks

    sent = land.at[pl.ds(0, rows), :]
    remote(b_ref, sent, near_send, near_recv.at[0], (partner, v)).wait_send()
    remote(b_ref, sent, inner_send, inner_recv.at[0], (o, v_inner)).wait_send()
    remote(b_ref, sent, outer_send, outer_recv.at[0], (o, v_outer)).wait_send()
    remote(sent, sent, far_send, far_recv.at[0], (relay_to, v)).wait_send()


def finish(total, land, amp_high, amp_low, out_ref, done, out_sem):
    rows, width = total.shape
    base, count = phases(rows)[-1]
    stores = []
    for k in range(width // CHUNK):
        where = pl.ds(k * CHUNK, CHUNK)
        block = land[pl.ds(STREAMS * base, STREAMS * count), where]
        done[:, where] = total[:, where] + spread(amp_high, amp_low, block)
        stores.append(pltpu.make_async_copy(done.at[:, where], out_ref.at[:, where], out_sem.at[k]))
        stores[-1].start()
    for store in stores:
        store.wait()


def local(b_factors, occ_energy, vir_energy):
    occ_block, vir_block, width = b_factors.shape
    occ_count = lax.axis_size("occ")
    vir_count = lax.axis_size("vir")
    rows = occ_block * vir_block
    plan = phases(rows)
    chunks = width // CHUNK
    short = min(count for _, count in plan)
    far = sum(chunks if count == short else chunks // WIDE for _, count in plan)
    block = pltpu.VMEM((rows, width), jnp.float32)
    half = pltpu.VMEM((rows, width), jnp.bfloat16)
    square = pltpu.VMEM((rows, rows), jnp.float32)
    amp = pltpu.VMEM((rows, rows), jnp.bfloat16)
    vmem = pl.BlockSpec(memory_space=pltpu.VMEM)
    smem = pl.BlockSpec(memory_space=pltpu.SMEM)
    hbm = pl.BlockSpec(memory_space=pl.ANY)
    sems = [pltpu.SemaphoreType.DMA((chunks // WIDE,))] + [pltpu.SemaphoreType.DMA] * 4 + [
        pltpu.SemaphoreType.DMA((count,))
        for count in (2 * AHEAD, far, len(plan), len(plan) * chunks // WIDE)]
    parts = pl.pallas_call(
        functools.partial(kernel, occ_count, vir_count, occ_block, vir_block),
        out_shape=[block, pltpu.VMEM((STREAMS * rows, width), jnp.float32), amp, amp],
        in_specs=[smem, smem, hbm],
        out_specs=[vmem] * 4,
        scratch_shapes=[
            block, half, half, square, square, pltpu.VMEM((len(plan), 8, rows), jnp.float32)] + sems,
        compiler_params=pltpu.CompilerParams(
            collective_id=0, has_side_effects=True, vmem_limit_bytes=42 * 2**20),
    )(occ_energy, vir_energy, b_factors.reshape(rows, width))
    out = pl.pallas_call(
        finish,
        out_shape=jax.ShapeDtypeStruct((rows, width), jnp.float32),
        in_specs=[vmem] * 4,
        out_specs=hbm,
        scratch_shapes=[block, pltpu.SemaphoreType.DMA((chunks,))],
        compiler_params=pltpu.CompilerParams(vmem_limit_bytes=10 * 2**20),
    )(*parts)
    return out.reshape(occ_block, vir_block, width)


def solution(mesh):
    in_specs = (P("occ", "vir", None), P(), P())
    out_specs = P("occ", "vir", None)
    return jax.shard_map(local, mesh=mesh, in_specs=in_specs, out_specs=out_specs, check_vma=False)
```

time: 110 us -> 104 us (0.945)
  Pallas kernels: 110 us -> 104 us
    pallas_call x1, Pallas kernels: 107 us -> 101 us  [local(): pl.pallas_call(functools.partial(kernel, occ_count, vir_count, occ_block,...]
where the time goes in v2:
time: 104 us
  Pallas kernels  104 us (100%)
    pallas_call x1, Pallas kernels, local(): pl.pallas_call(functools.partial(kernel, occ_count, vir_count, occ_block,...  101 us
    pallas_call x1, Pallas kernels, local(): pl.pallas_call(finish, out_shape=jax.ShapeDtypeStruct((rows, width), jnp....  2.38 us

profile of v2, /device:TPU:0, one launch (start us, length us, event | category | flops | bytes accessed | tf_op | source)
XLA Modules:
  0.0 103.8 jit_solution(9592470601160729625)
XLA Ops:
  0.0 101.4 %shard_map.37 = (f32[256,4096]{1,0:T(8,128)S(1)}, f32[1024,4096]{1,0:T(8,128)S(1)}, bf16[256,256]{1,0:T(8,128)(2,1)S(1)}, bf16[256,256]{1,0:T(8,128)(2,1)S(1)}) custom-call(f32[32]{0:T(128)} %occ_ref.1, f32[256]{0:T(256)} %vir_ref.1, f32[256,4096]{1,0:T(8,128)} %bitcast.2), custom_call_target="tpu_custom_call" | custom-call | tf_op jit(solution)/shard_map/pallas_call | solution.py:325
  101.4 2.4 %shard_map.38 = f32[256,4096]{1,0:T(8,128)} custom-call(f32[256,4096]{1,0:T(8,128)S(1)} %get-tuple-element.9.total, f32[1024,4096]{1,0:T(8,128)S(1)} %get-tuple-element.10.land, bf16[256,256]{1,0:T(8,128)(2,1)S(1)} %get-tuple-element.11.amp_high, bf16[256,256]{1,0:T(8,128)(2,1)S(1)} %get-tuple-element.12.amp_low), custom_call_target="tpu_custom_call" | custom-call | tf_op jit(solution)/shard_map/pallas_call | solution.py:335

commit v3 on v2

--- a/solution.py
+++ b/solution.py
@@ -11,9 +11,10 @@
 CHUNK = 512
 STREAMS = 4
 SHARES = (4, 4, 4, 8, 8)
-LAG = 3
+LAG = 4
 RELAY_ROWS = 16
 AHEAD = 8
+EARLY = 0
 WIDE = 2
 DEPTH = 256
 
@@ -88,8 +89,8 @@
     pairs = [WIDE if count > min(c for _, c in plan) else 1 for _, count in plan]
     far_first = [sum(chunks // pair for pair in pairs[:p]) for p in range(len(plan))]
 
-    def mine(p, i, count, where):
-        return b_ref.at[pl.ds(plan[p][0] + i * count, count), where]
+    def mine(p, i, count, where, ref=b_ref):
+        return ref.at[pl.ds(plan[p][0] + i * count, count), where]
 
     def landed(p, stream, i, count, where):
         return land.at[pl.ds(STREAMS * plan[p][0] + stream * plan[p][1] + i * count, count), where]
@@ -98,9 +99,9 @@
         return pltpu.make_async_remote_copy(
             source, target, send_sem, recv_sem, device_id=device, device_id_type=MESH)
 
-    def near_copy(p, k, i):
-        return remote(
-            mine(p, i, RELAY_ROWS, cols(k)), landed(p, 0, i, RELAY_ROWS, cols(k)),
+    def near_copy(p, k, i, ref=b_ref):
+        return remote(
+            mine(p, i, RELAY_ROWS, cols(k), ref), landed(p, 0, i, RELAY_ROWS, cols(k)),
             near_send, near_recv.at[lax.rem(k * pieces[p] + i, 2 * AHEAD)], (partner, v))
 
     def far_copy(p, k, i):
@@ -132,14 +133,14 @@
     barrier = pltpu.get_barrier_semaphore()
     for device in ((partner, v), (relay_to, v), (relay_from, v), (o, v_inner), (o, v_outer)):
         pl.semaphore_signal(barrier, inc=1, device_id=device, device_id_type=MESH)
+    every(chunks // WIDE, lambda k: load(k).start())
+    load(0).wait()
     pl.semaphore_wait(barrier, 5)
     for n in range(AHEAD):
-        near_copy(0, n // pieces[0], n % pieces[0]).start()
+        near_copy(0, n // pieces[0], n % pieces[0], own).start()
     for p in range(len(plan)):
         every(chunks // WIDE, lambda c: outer_copy(p, c).start())
         inner_copy(p).start()
-        if p == 0:
-            every(chunks // WIDE, lambda k: load(k).start())
 
     lane = lax.broadcasted_iota(jnp.int32, (8, rows), 1)
 
@@ -182,9 +183,6 @@
     sums[...] = jnp.zeros_like(sums)
 
     def own_chunk(k):
-        @pl.when(lax.rem(k, WIDE) == 0)
-        def _():
-            load(k // WIDE).wait()
         high, low = split(own[:, cols(k)])
         own_high[:, cols(k)] = high
         own_low[:, cols(k)] = low
@@ -220,14 +218,14 @@
 
         @pl.when(k < later)
         def _():
-            near_copy(p, k + AHEAD // pieces[p], i).start()
+            near_copy(p, k + AHEAD // pieces[p], i, own).start()
 
         if p + 1 < len(plan):
             ratio = pieces[p] // pieces[p + 1]
 
             @pl.when(k >= later)
             def _():
-                near_copy(p + 1, (k - later) * ratio + i // pieces[p + 1], i % pieces[p + 1]).start()
+                near_copy(p + 1, (k - later) * ratio + i // pieces[p + 1], i % pieces[p + 1], own).start()
 
     def arrive(p, k, work):
         for i in range(pieces[p]):
@@ -238,12 +236,13 @@
     def fill(p):
         gaps[p] = gap_row(plan[p][0], plan[p][1], sources)
 
-    assert pieces[0] == 4 and len(plan) == 5
-    half = chunks // 2
-    every(half, own_chunk)
-    arrive(0, 0, [functools.partial(every, half + n + 1, own_chunk, half + n) for n in range(half)])
-    arrive(0, 1, [lambda: amplitude(own_row, rows), lambda: fill(0), lambda: fill(1)])
-    arrive(0, 2, [lambda: fill(2), lambda: fill(3), lambda: fill(4)])
+    every(chunks // WIDE, lambda k: load(k).wait(), 1)
+    every(EARLY, own_chunk)
+    slots = [functools.partial(every, k + 1, own_chunk, k) for k in range(EARLY, chunks)]
+    slots += [lambda: amplitude(own_row, rows)] + [functools.partial(fill, p) for p in range(len(plan))]
+    for k in range(LAG):
+        arrive(0, k, slots[k * pieces[0]:(k + 1) * pieces[0]])
+    assert len(slots) <= LAG * pieces[0]
 
     done, runs = 0, []
     for p in range(len(plan)):

time: 104 us -> 103 us (level)
  no operation moved by 1% of the time
where the time goes in v3:
time: 103 us
  Pallas kernels  103 us (100%)
    pallas_call x1, Pallas kernels, local(): pl.pallas_call(functools.partial(kernel, occ_count, vir_count, occ_block,...  101 us
    pallas_call x1, Pallas kernels, local(): pl.pallas_call(finish, out_shape=jax.ShapeDtypeStruct((rows, width), jnp....  2.37 us

profile of v3, /device:TPU:0, one launch (start us, length us, event | category | flops | bytes accessed | tf_op | source)
XLA Modules:
  0.0 103.1 jit_solution(16308327049083907112)
XLA Ops:
  0.0 100.7 %shard_map.37 = (f32[256,4096]{1,0:T(8,128)S(1)}, f32[1024,4096]{1,0:T(8,128)S(1)}, bf16[256,256]{1,0:T(8,128)(2,1)S(1)}, bf16[256,256]{1,0:T(8,128)(2,1)S(1)}) custom-call(f32[32]{0:T(128)} %occ_ref.1, f32[256]{0:T(256)} %vir_ref.1, f32[256,4096]{1,0:T(8,128)} %bitcast.2), custom_call_target="tpu_custom_call" | custom-call | tf_op jit(solution)/shard_map/pallas_call | solution.py:324
  100.7 2.4 %shard_map.38 = f32[256,4096]{1,0:T(8,128)} custom-call(f32[256,4096]{1,0:T(8,128)S(1)} %get-tuple-element.9.total, f32[1024,4096]{1,0:T(8,128)S(1)} %get-tuple-element.10.land, bf16[256,256]{1,0:T(8,128)(2,1)S(1)} %get-tuple-element.11.amp_high, bf16[256,256]{1,0:T(8,128)(2,1)S(1)} %get-tuple-element.12.amp_low), custom_call_target="tpu_custom_call" | custom-call | tf_op jit(solution)/shard_map/pallas_call | solution.py:334

commit v4 on v3

--- a/solution.py
+++ b/solution.py
@@ -11,10 +11,9 @@
 CHUNK = 512
 STREAMS = 4
 SHARES = (4, 4, 4, 8, 8)
-LAG = 4
+LAG = 5
 RELAY_ROWS = 16
 AHEAD = 8
-EARLY = 0
 WIDE = 2
 DEPTH = 256
 
@@ -69,7 +68,7 @@
     occ_count, vir_count, occ_block, vir_block,
     occ_ref, vir_ref, b_ref, total, land, amp_high, amp_low,
     own, own_high, own_low, sums, mine_gap, gaps,
-    own_sem, near_send, far_send, inner_send, outer_send, near_recv, far_recv, inner_recv, outer_recv,
+    far_free, own_sem, near_send, far_send, inner_send, outer_send, near_recv, far_recv, inner_recv, outer_recv,
 ):
     rows, width = b_ref.shape
     plan = phases(rows)
@@ -87,7 +86,9 @@
     sources = ((partner, v), (o, v_inner), (o, v_outer), (across, v))
     pieces = [count // RELAY_ROWS for _, count in plan]
     pairs = [WIDE if count > min(c for _, c in plan) else 1 for _, count in plan]
-    far_first = [sum(chunks // pair for pair in pairs[:p]) for p in range(len(plan))]
+    far_first = [sum(chunks // pair for pair in pairs[:p]) for p in range(len(plan) + 1)]
+    reused = far_first[-1] - chunks
+    assert chunks in far_first and reused in far_first
 
     def mine(p, i, count, where, ref=b_ref):
         return ref.at[pl.ds(plan[p][0] + i * count, count), where]
@@ -107,13 +108,13 @@
     def far_copy(p, k, i):
         return remote(
             landed(p, 0, i, RELAY_ROWS, cols(k)), landed(p, 3, i, RELAY_ROWS, cols(k)),
-            far_send, far_recv.at[far_first[p] + k // pairs[p]], (relay_to, v))
+            far_send, far_recv.at[lax.rem(far_first[p] + k // pairs[p], chunks)], (relay_to, v))
 
     def far_here(p, c):
         where = cols(c, pairs[p])
         return remote(
             landed(p, 0, 0, plan[p][1], where), landed(p, 3, 0, plan[p][1], where),
-            far_send, far_recv.at[far_first[p] + c], (relay_to, v))
+            far_send, far_recv.at[lax.rem(far_first[p] + c, chunks)], (relay_to, v))
 
     def inner_copy(p):
         count = plan[p][1]
@@ -198,13 +199,18 @@
             total[:, cols(k)] += spread(amp_high, amp_low, block(p - 1, k))
 
     def read_second(p, k):
+        def take_far(c):
+            far_here(p, c).wait_recv()
+            if far_first[p] < reused:
+                pl.semaphore_signal(far_free, inc=1, device_id=(relay_from, v), device_id_type=MESH)
+
         if pairs[p] == 1:
-            far_here(p, k).wait_recv()
+            take_far(k)
 
         @pl.when(lax.rem(k, WIDE) == 0)
         def _():
             if pairs[p] == WIDE:
-                far_here(p, k // WIDE).wait_recv()
+                take_far(k // WIDE)
             outer_copy(p, k // WIDE).wait_recv()
         gather(block(p, k), k)
 
@@ -213,6 +219,10 @@
 
     def relay(p, k, i):
         near_copy(p, k, i).wait_recv()
+        if i == 0 and far_first[p] >= chunks:
+            @pl.when(lax.rem(k, pairs[p]) == 0)
+            def _():
+                pl.semaphore_wait(far_free, 1)
         far_copy(p, k, i).start()
         later = chunks - AHEAD // pieces[p]
 
@@ -237,8 +247,8 @@
         gaps[p] = gap_row(plan[p][0], plan[p][1], sources)
 
     every(chunks // WIDE, lambda k: load(k).wait(), 1)
-    every(EARLY, own_chunk)
-    slots = [functools.partial(every, k + 1, own_chunk, k) for k in range(EARLY, chunks)]
+
+    slots = [functools.partial(every, k + 1, own_chunk, k) for k in range(chunks)]
     slots += [lambda: amplitude(own_row, rows)] + [functools.partial(fill, p) for p in range(len(plan))]
     for k in range(LAG):
         arrive(0, k, slots[k * pieces[0]:(k + 1) * pieces[0]])
@@ -309,8 +319,6 @@
     rows = occ_block * vir_block
     plan = phases(rows)
     chunks = width // CHUNK
-    short = min(count for _, count in plan)
-    far = sum(chunks if count == short else chunks // WIDE for _, count in plan)
     block = pltpu.VMEM((rows, width), jnp.float32)
     half = pltpu.VMEM((rows, width), jnp.bfloat16)
     square = pltpu.VMEM((rows, rows), jnp.float32)
@@ -318,9 +326,9 @@
     vmem = pl.BlockSpec(memory_space=pltpu.VMEM)
     smem = pl.BlockSpec(memory_space=pltpu.SMEM)
     hbm = pl.BlockSpec(memory_space=pl.ANY)
-    sems = [pltpu.SemaphoreType.DMA((chunks // WIDE,))] + [pltpu.SemaphoreType.DMA] * 4 + [
+    sems = [pltpu.SemaphoreType.REGULAR, pltpu.SemaphoreType.DMA((chunks // WIDE,))] + [pltpu.SemaphoreType.DMA] * 4 + [
         pltpu.SemaphoreType.DMA((count,))
-        for count in (2 * AHEAD, far, len(plan), len(plan) * chunks // WIDE)]
+        for count in (2 * AHEAD, chunks, len(plan), len(plan) * chunks // WIDE)]
     parts = pl.pallas_call(
         functools.partial(kernel, occ_count, vir_count, occ_block, vir_block),
         out_shape=[block, pltpu.VMEM((STREAMS * rows, width), jnp.float32), amp, amp],

time: 103 us -> 103 us (level)
  no operation moved by 1% of the time
where the time goes in v4:
time: 103 us
  Pallas kernels  103 us (100%)
    pallas_call x1, Pallas kernels, local(): pl.pallas_call(functools.partial(kernel, occ_count, vir_count, occ_block,...  101 us
    pallas_call x1, Pallas kernels, local(): pl.pallas_call(finish, out_shape=jax.ShapeDtypeStruct((rows, width), jnp....  2.37 us

profile of v4, /device:TPU:0, one launch (start us, length us, event | category | flops | bytes accessed | tf_op | source)
XLA Modules:
  0.0 102.9 jit_solution(7926430816664711072)
XLA Ops:
  0.0 100.6 %shard_map.37 = (f32[256,4096]{1,0:T(8,128)S(1)}, f32[1024,4096]{1,0:T(8,128)S(1)}, bf16[256,256]{1,0:T(8,128)(2,1)S(1)}, bf16[256,256]{1,0:T(8,128)(2,1)S(1)}) custom-call(f32[32]{0:T(128)} %occ_ref.1, f32[256]{0:T(256)} %vir_ref.1, f32[256,4096]{1,0:T(8,128)} %bitcast.2), custom_call_target="tpu_custom_call" | custom-call | tf_op jit(solution)/shard_map/pallas_call | solution.py:332
  100.6 2.4 %shard_map.38 = f32[256,4096]{1,0:T(8,128)} custom-call(f32[256,4096]{1,0:T(8,128)S(1)} %get-tuple-element.9.total, f32[1024,4096]{1,0:T(8,128)S(1)} %get-tuple-element.10.land, bf16[256,256]{1,0:T(8,128)(2,1)S(1)} %get-tuple-element.11.amp_high, bf16[256,256]{1,0:T(8,128)(2,1)S(1)} %get-tuple-element.12.amp_low), custom_call_target="tpu_custom_call" | custom-call | tf_op jit(solution)/shard_map/pallas_call | solution.py:342

commit v5 on v4

--- a/solution.py
+++ b/solution.py
@@ -129,7 +129,7 @@
             outer_send, outer_recv.at[p * (chunks // WIDE) + c], (o, v_outer))
 
     def load(k):
-        return pltpu.make_async_copy(b_ref.at[:, cols(k, WIDE)], own.at[:, cols(k, WIDE)], own_sem.at[k])
+        return pltpu.make_async_copy(b_ref.at[:, cols(k, WIDE)], own.at[:, cols(k, WIDE)], own_sem.at[jnp.minimum(k, 1)])
 
     barrier = pltpu.get_barrier_semaphore()
     for device in ((partner, v), (relay_to, v), (relay_from, v), (o, v_inner), (o, v_outer)):
@@ -171,7 +171,7 @@
         mine = (own_high[:, cols(k)], own_low[:, cols(k)])
         sums[:, :count] += product(mine, split(block), (1, 1))
 
-    def amplitude(row, count):
+    def amplitude(row, count, last=False):
         value = sums[:, :count] / (mine_gap[:, :count] + whole(row)[:, :count])
         high, low = split(value)
         amp_high[:, :count] = high
@@ -179,7 +179,8 @@
             amp_high[:, count:2 * count] = low
         else:
             amp_low[:, :count] = low
-        sums[...] = jnp.zeros_like(sums)
+        if not last:
+            sums[...] = jnp.zeros_like(sums)
 
     sums[...] = jnp.zeros_like(sums)
 
@@ -215,7 +216,7 @@
         gather(block(p, k), k)
 
     def finished(p):
-        amplitude(gaps[p], STREAMS * plan[p][1])
+        amplitude(gaps[p], STREAMS * plan[p][1], p == len(plan) - 1)
 
     def relay(p, k, i):
         near_copy(p, k, i).wait_recv()
@@ -246,7 +247,8 @@
     def fill(p):
         gaps[p] = gap_row(plan[p][0], plan[p][1], sources)
 
-    every(chunks // WIDE, lambda k: load(k).wait(), 1)
+    others = pl.ds(WIDE * CHUNK, width - WIDE * CHUNK)
+    pltpu.make_async_copy(b_ref.at[:, others], own.at[:, others], own_sem.at[1]).wait()
 
     slots = [functools.partial(every, k + 1, own_chunk, k) for k in range(chunks)]
     slots += [lambda: amplitude(own_row, rows)] + [functools.partial(fill, p) for p in range(len(plan))]
@@ -326,7 +328,7 @@
     vmem = pl.BlockSpec(memory_space=pltpu.VMEM)
     smem = pl.BlockSpec(memory_space=pltpu.SMEM)
     hbm = pl.BlockSpec(memory_space=pl.ANY)
-    sems = [pltpu.SemaphoreType.REGULAR, pltpu.SemaphoreType.DMA((chunks // WIDE,))] + [pltpu.SemaphoreType.DMA] * 4 + [
+    sems = [pltpu.SemaphoreType.REGULAR, pltpu.SemaphoreType.DMA((2,))] + [pltpu.SemaphoreType.DMA] * 4 + [
         pltpu.SemaphoreType.DMA((count,))
         for count in (2 * AHEAD, chunks, len(plan), len(plan) * chunks // WIDE)]
     parts = pl.pallas_call(

time: 103 us -> 103 us (level)
  no operation moved by 1% of the time
where the time goes in v5:
time: 103 us
  Pallas kernels  103 us (100%)
    pallas_call x1, Pallas kernels, local(): pl.pallas_call(functools.partial(kernel, occ_count, vir_count, occ_block,...  101 us
    pallas_call x1, Pallas kernels, local(): pl.pallas_call(finish, out_shape=jax.ShapeDtypeStruct((rows, width), jnp....  2.37 us

profile of v5, /device:TPU:0, one launch (start us, length us, event | category | flops | bytes accessed | tf_op | source)
XLA Modules:
  0.0 102.9 jit_solution(10954067724977587741)
XLA Ops:
  0.0 100.5 %shard_map.37 = (f32[256,4096]{1,0:T(8,128)S(1)}, f32[1024,4096]{1,0:T(8,128)S(1)}, bf16[256,256]{1,0:T(8,128)(2,1)S(1)}, bf16[256,256]{1,0:T(8,128)(2,1)S(1)}) custom-call(f32[32]{0:T(128)} %occ_ref.1, f32[256]{0:T(256)} %vir_ref.1, f32[256,4096]{1,0:T(8,128)} %bitcast.2), custom_call_target="tpu_custom_call" | custom-call | tf_op jit(solution)/shard_map/pallas_call | solution.py:334
  100.5 2.4 %shard_map.38 = f32[256,4096]{1,0:T(8,128)} custom-call(f32[256,4096]{1,0:T(8,128)S(1)} %get-tuple-element.9.total, f32[1024,4096]{1,0:T(8,128)S(1)} %get-tuple-element.10.land, bf16[256,256]{1,0:T(8,128)(2,1)S(1)} %get-tuple-element.11.amp_high, bf16[256,256]{1,0:T(8,128)(2,1)S(1)} %get-tuple-element.12.amp_low), custom_call_target="tpu_custom_call" | custom-call | tf_op jit(solution)/shard_map/pallas_call | solution.py:344
